TPU v7x, 32 devices: a whole 2x2x4 slice. The times are simulated.
32 devices in a mesh: lat: 8 (over z, y), lev: 4 (over x, core).
Axes of the slice: x: 2, y: 2, z: 4, core: 2. Of those that a mesh axis runs over, the one named last changes fastest.
Arguments:
- assign: int32 [640], replicated, may hold values from 0 to 639, each once
- u_spec: bfloat16 [640, 32, 2, 640], P('lat', 'lev'), may hold values from -0.25 to 0.25
- v_spec: bfloat16 [640, 32, 2, 640], P('lat', 'lev'), may hold values from -0.25 to 0.25
- basis: bfloat16 [640, 640, 640], P('lat', 'lev'), may hold values from -0.25 to 0.25
Outputs:
- vort_spec: float32 [640, 32, 2, 640], P('lat', 'lev')
Inputs may be any that keep to these rules, and one draw needn't show every extreme that they name: Row k of u_spec, v_spec, basis and vort_spec belongs to zonal wavenumber assign[k]; each of the 640 wavenumbers appears once.
All inputs are finite; a program needn't handle non-finite values.
Results may differ from a plain program's by a relative error of at most 0.0061.
Values may be sent and summed in bfloat16 or wider, within the bound.
A program may use at most 256 MiB of HBM per device.

v0:
```python
import math

import jax
import jax.numpy as jnp
from jax import lax
from jax.sharding import PartitionSpec as P

M = 640
LAT = 1280
LON = 2560


def padded_2(block, sides, width):
    for axis, dim in sides:
        count = lax.axis_size(axis)
        forward = [(i, i + 1) for i in range(count - 1)]
        backward = [(target, source) for source, target in forward]
        low = lax.ppermute(
            lax.slice_in_dim(block, block.shape[dim] - width, None, axis=dim), axis, forward
        )
        high = lax.ppermute(lax.slice_in_dim(block, 0, width, axis=dim), axis, backward)
        block = jnp.concatenate([low, block, high], axis=dim)
    return block


def degree_factors(wavenums):
    degree = jnp.arange(M, dtype=jnp.int32)
    live_mask = (degree[None, :] >= wavenums[:, None]).astype(jnp.int32)
    parity = 1 - 2 * ((degree[None, :] + wavenums[:, None]) % 2)
    return (live_mask, live_mask * parity)


def zonal_tables(wavenums):
    columns = jnp.arange(LON, dtype=jnp.int32)
    phases = wavenums[:, None] * columns[None, :] % LON
    angles = phases.astype(jnp.float32) * (2.0 * math.pi / LON)
    return jnp.stack([jnp.cos(angles), jnp.sin(angles)], axis=0).astype(jnp.bfloat16)


def body(assign, u_spec, v_spec, basis):
    slot_count = u_spec.shape[0]
    lev_dev = u_spec.shape[1]
    lat_count = lax.axis_size("lat")
    half_rows = LAT // 2
    row_count = LAT // lat_count
    lat_index = lax.axis_index("lat")
    my_waves = lax.dynamic_slice_in_dim(assign, lat_index * slot_count, slot_count)
    live_mask, signed = degree_factors(my_waves)
    live_half = live_mask.astype(jnp.bfloat16)[:, None, :]
    signed_half = signed.astype(jnp.bfloat16)[:, None, :]
    live_full = live_mask.astype(jnp.float32)[:, None, :]
    signed_full = signed.astype(jnp.float32)[:, None, :]
    basis_all = lax.all_gather(basis, "lev", axis=1, tiled=True)
    spectra = jnp.stack([u_spec, v_spec], axis=2).reshape(slot_count, lev_dev * 4, M)
    northern = jnp.einsum(
        "kcn,kjn->kcj", spectra * live_half, basis_all, preferred_element_type=jnp.float32
    )
    southern = jnp.einsum(
        "kcn,kjn->kcj", spectra * signed_half, basis_all, preferred_element_type=jnp.float32
    )[:, :, ::-1]
    fourier = jnp.concatenate([northern, southern], axis=2).astype(jnp.bfloat16)
    incoming = lax.all_to_all(fourier, "lat", split_axis=2, concat_axis=0, tiled=True)
    incoming = incoming.reshape(M, lev_dev, 2, 2, row_count)
    zonal_table = zonal_tables(assign)
    grid_fields = jnp.einsum(
        "klfcj,ckq->fljq", incoming, zonal_table, preferred_element_type=jnp.float32
    )
    scaled = grid_fields[0]
    padded = padded_2(scaled, (("lat", 1),), 1)
    upper_row = jnp.where(lat_index == 0, -jnp.roll(scaled[:, 0], LON // 2, axis=-1), padded[:, 0])
    lower_row = jnp.where(
        lat_index == lat_count - 1, -jnp.roll(scaled[:, -1], LON // 2, axis=-1), padded[:, -1]
    )
    row_above = jnp.concatenate([upper_row[:, None], scaled[:, :-1]], axis=1)
    row_below = jnp.concatenate([scaled[:, 1:], lower_row[:, None]], axis=1)
    merid_v = grid_fields[1]
    vorticity = 0.5 * (jnp.roll(merid_v, -1, axis=-1) - jnp.roll(merid_v, 1, axis=-1)) - 0.5 * (
        row_above - row_below
    )
    flux = (vorticity * scaled).astype(jnp.bfloat16)
    zonal_back = jnp.einsum(
        "ljq,ckq->klcj", flux, zonal_table, preferred_element_type=jnp.float32
    ) * (1.0 / math.sqrt(LON))
    zonal_back = zonal_back.astype(jnp.bfloat16).reshape(M, lev_dev * 2, row_count)
    returned = lax.all_to_all(zonal_back, "lat", split_axis=0, concat_axis=2, tiled=True)
    northern = jnp.einsum(
        "kjn,kcj->kcn", basis_all, returned[:, :, :half_rows], preferred_element_type=jnp.float32
    )
    southern = jnp.einsum(
        "kjn,kcj->kcn",
        basis_all,
        returned[:, :, half_rows:][:, :, ::-1],
        preferred_element_type=jnp.float32,
    )
    combined = live_full * northern + signed_full * southern
    result = combined.reshape(slot_count, lev_dev, 2, M)
    return result


def solution(mesh):
    return jax.shard_map(
        body,
        mesh=mesh,
        in_specs=(
            P(),
            P("lat", "lev", None, None),
            P("lat", "lev", None, None),
            P("lat", "lev", None),
        ),
        out_specs=P("lat", "lev", None, None),
        check_vma=False,
    )
```

profile of v0, /device:TPU:0, one launch (start us, length us, event | category | flops | bytes accessed | tf_op | source)
XLA Modules:
  0.0 1042.3 jit_solution(14617941247939574557)
XLA Ops:
  9.5 0.9 fusion.36
  11.2 3.7 bitcast_multiply_fusion.1
  14.9 380.5 %all-gather.2.cloned.1.call-done = bf16[80,640,640]{2,1,0:T(8,128)(2,1)} async-done(((bf16[80,160,640]{2,1,0:T(8,128)(2,1)}), bf16[80,640,640]{2,1,0:T(8,128)(2,1)}) %all-gather.2.cloned.1.call-update) | async-done | bytes 65536016 | tf_op jit(solution)/shard_map/all_gather | solution.py:53
  395.4 26.9 %fusion.16 = bf16[80,32,640]{2,1,0:T(8,128)(2,1)S(1)} fusion(bf16[80,640,640]{2,1,0:T(8,128)(2,1)} %all-gather.2.cloned.1.call-done, bf16[80,32,640]{2,0,1:T(8,128)(2,1)} %get-tuple-element.16), kind=kOutput, calls=%fused_computation.31 | convolution fusion | flops 2097152000 | bytes 72089600 | tf_op jit(solution)/shard_map/kcn,kjn->kcj/dot_general | solution.py:58
  422.3 7.3 rev.6
  429.6 26.9 %fusion.24 = bf16[80,32,640]{2,1,0:T(8,128)(2,1)S(1)} fusion(bf16[80,640,640]{2,1,0:T(8,128)(2,1)} %all-gather.2.cloned.1.call-done, bf16[80,32,640]{2,0,1:T(8,128)(2,1)} %get-tuple-element.15), kind=kOutput, calls=%fused_computation.36 | convolution fusion | flops 2098790400 | bytes 72089600 | tf_op jit(solution)/shard_map/kcn,kjn->kcj/dot_general | solution.py:55
  456.5 5.4 pad_maximum_fusion.1
  461.9 16.3 %copy.39 = bf16[80,32,1280]{0,1,2:T(8,128)(2,1)} copy(bf16[80,32,1280]{2,1,0:T(8,128)(2,1)} %pad_maximum_fusion.1) | data formatting | bytes 13107200 | tf_op jit(solution)/shard_map/concatenate | solution.py:61
  478.3 5.7 all-to-all-start
  484.0 28.8 %cosine_convert_fusion = (bf16[1,640,2560]{2,1,0:T(8,128)(2,1)S(1)}, bf16[1,640,2560]{2,1,0:T(8,128)(2,1)}) fusion(s32[640]{0:T(1024)S(1)} %copy-done.4), kind=kLoop, calls=%fused_computation.22 | loop fusion | flops 18022400 | bytes 6556160 | tf_op jit(solution)/shard_map/convert.2
  512.8 199.6 %all-to-all-done = bf16[80,32,1280]{0,1,2:T(8,128)(2,1)} async-done(((bf16[80,32,1280]{0,1,2:T(8,128)(2,1)}), bf16[80,32,1280]{0,1,2:T(8,128)(2,1)}, u32[]{:S(2)}, u32[]{:S(2)}) %all-to-all-start) | async-done | bytes 6553632 | tf_op jit(solution)/shard_map/all_to_all | solution.py:62
  712.5 14.8 %copy.70 = bf16[80,32,8,160]{0,2,3,1:T(8,128)(2,1)} copy(bf16[80,32,8,160]{0,1,3,2:T(8,128)(2,1)} %bitcast.7) | data formatting | bytes 13107200 | tf_op jit(solution)/shard_map/all_to_all | solution.py:62
  727.2 15.8 %reshape.253 = bf16[640,8,2,2,160]{0,4,3,2,1:T(8,128)(2,1)} reshape(bf16[8,80,32,160]{1,0,3,2:T(8,128)(2,1)} %bitcast.74) | data formatting | bytes 13107200 | tf_op jit(solution)/shard_map/reshape | solution.py:63
  743.0 23.1 %convolution_bitcast_fusion = f32[2,8,160,2560]{3,2,0,1:T(8,128)} fusion(bf16[640,8,2,2,160]{0,4,3,2,1:T(8,128)(2,1)} %reshape.253, bf16[1,640,2560]{2,1,0:T(8,128)(2,1)} %get-tuple-element.24, bf16[1,640,2560]{2,1,0:T(8,128)(2,1)S(1)} %get-tuple-element.23), kind=kOutput, calls=%fused_computation.9 | convolution fusion | flops 16790323200 | bytes 39321600 | tf_op jit(solution)/shard_map/klfcj,ckq->fljq/dot_general | solution.py:65
  766.1 9.3 slice_bitcast_fusion.1
  775.5 1.3 collective-permute-start.1
  776.8 9.2 fusion.45
  786.0 4.6 collective-permute-start
  790.6 9.9 fusion.43
  800.6 1.3 fusion.44
  802.1 26.4 %fusion.15 = bf16[640,8,2,160]{0,3,1,2:T(8,128)(2,1)} fusion(f32[8,1,2560]{2,1,0:T(1,128)S(1)} %broadcast_select_fusion, f32[8,159,2560]{2,1,0:T(8,128)} %get-tuple-element.12, f32[8,159,2560]{2,1,0:T(8,128)} %get-tuple-element.11, f32[8,1,2560]{2,1,0:T(1,128)S(1)} %copy.43, f32[8,160,2559]{2,1,0:T(8,128)} %get-tuple-element.8, ...), kind=kOutput, calls=%fused_computation.27 | convolution fusion | flops 8441036800 | bytes 76840960 | tf_op jit(solution)/shard_map/ljq,ckq->klcj/dot_general | solution.py:81
  828.5 2.3 copy.45
  830.8 6.6 copy.46
  837.3 119.3 %all_to_all.33 = bf16[640,16,160]{2,1,0:T(8,128)(2,1)S(1)} all-to-all(bf16[640,16,160]{2,1,0:T(8,128)(2,1)} %copy.46), channel_id=1, replica_groups=mesh['lat'=8,'lev'=4] {'lat'}, dimensions={0} | all-to-all | bytes 6553600 | tf_op jit(solution)/shard_map/all_to_all | solution.py:85
  956.7 8.0 copy.48
  964.6 8.0 all_to_all.30
  972.6 1.4 slice.87
  974.0 0.8 copy-done
  974.9 6.9 rev.7
  981.8 22.6 %fusion.27 = f32[80,16,640]{2,1,0:T(8,128)S(1)} fusion(bf16[80,640,640]{2,1,0:T(8,128)(2,1)} %all-gather.2.cloned.1.call-done, bf16[80,16,1280]{2,1,0:T(8,128)(2,1)} %copy-done), kind=kOutput, calls=%fused_computation.37 | convolution fusion | flops 1048576000 | bytes 70451200 | tf_op jit(solution)/shard_map/kjn,kcj->kcn/dot_general | solution.py:86
  1004.4 25.4 %multiply_add_fusion = f32[80,16,640]{2,1,0:T(8,128)} fusion(f32[80,16,640]{2,1,0:T(8,128)S(1)} %fusion.27, bf16[80,16,640]{2,1,0:T(8,128)(2,1)} %rev.7, bf16[80,640,640]{2,1,0:T(8,128)(2,1)} %all-gather.2.cloned.1.call-done, f32[80,640]{1,0:T(8,128)S(1)} %copy-done.3, f32[80,640]{1,0:T(8,128)} %get-tuple-element.25), kind=kOutput, calls=%fused_computation.35 | convolution fusion | flops 1051033600 | bytes 74137600 | tf_op jit(solution)/shard_map/kjn,kcj->kcn/dot_general | solution.py:89
  1029.8 5.2 reshape.255
  (26 shorter events, 4.1 us)
Async XLA Ops:
  6.5 0.7 copy-start.4
  6.5 1.4 copy-start.1
  6.5 1.9 copy-start.2
  6.5 388.9 %all-gather.2.cloned.1.call-start = ((), (), s32[]{:S(2)}) async-start(), calls=%async_computation.2 | async-start | bytes 81920000 | tf_op jit(solution)/shard_map/all_gather | solution.py:53
  478.3 234.2 %all-to-all-start = ((bf16[80,32,1280]{0,1,2:T(8,128)(2,1)}), bf16[80,32,1280]{0,1,2:T(8,128)(2,1)}, u32[]{:S(2)}, u32[]{:S(2)}) async-start(bf16[80,32,1280]{0,1,2:T(8,128)(2,1)} %copy.39), calls=%async_computation | async-start | bytes 20971520 | tf_op jit(solution)/shard_map/all_to_all | solution.py:62
  775.5 26.4 %collective-permute-start.1 = (f32[8,1,2560]{2,1,0:T(1,128)S(1)}, f32[8,1,2560]{2,1,0:T(1,128)S(1)}, u32[]{:S(2)}, u32[]{:S(2)}) collective-permute-start(f32[8,1,2560]{2,1,0:T(1,128)S(1)} %get-tuple-element.14), channel_id=1, source_target_pairs={{4,0},{8,4},{12,8},{16,12},{20,16},{24,20},{28,24},{5,1},{9,5},{13... | collective-permute-start | bytes 245768 | tf_op jit(solution)/shard_map/ppermute | solution.py:21
  786.0 15.8 %collective-permute-start = (f32[8,1,2560]{2,0,1:T(8,128)S(1)}, f32[8,1,2560]{2,0,1:T(8,128)S(1)}, u32[]{:S(2)}, u32[]{:S(2)}) collective-permute-start(f32[8,1,2560]{2,0,1:T(8,128)S(1)} %copy.72), channel_id=1, source_target_pairs={{0,4},{4,8},{8,12},{12,16},{16,20},{20,24},{24,28},{1,5},{5,9},{9,... | collective-permute-start | bytes 245768 | tf_op jit(solution)/shard_map/ppermute | solution.py:18
  972.6 2.2 copy-start
  981.8 22.7 %copy-start.3 = (f32[80,640]{1,0:T(8,128)S(1)}, f32[80,640]{1,0:T(8,128)}, u32[]{:S(2)}) copy-start(f32[80,640]{1,0:T(8,128)} %get-tuple-element.27) | copy-start | bytes 614404
Sparse Core Ops, SparseCore 0:
  8.9 386.4 all-gather.1
where the time goes:
time: 1050 us; the launch traced here: 1040 us
  waiting for transfers between devices  581 us (55%)
  matrix products  151 us (14%)
  local copies, waits for them, and re-layouts  125 us (12%)
  blocking collectives  119 us (11%)
  other arithmetic  40 us (4%)
  between operations  14 us (1%)
  starting transfers between devices  11.6 us (1%)
    all_gather x1, waiting for transfers between devices, body(): basis_all = lax.all_gather(basis, 'lev', axis=1, tiled=True)  381 us
    all_to_all x1, waiting for transfers between devices, body(): lax.all_to_all(fourier, 'lat', split_axis=2, concat_axis=0, tiled=True)  200 us
    all_to_all x1, blocking collectives, body(): lax.all_to_all(zonal_back, 'lat', split_axis=0, concat_axis=2, tiled=True)  119 us
    another operation x1, other arithmetic  28.8 us
    dot_general x1, matrix products, body(): jnp.einsum('kcn,kjn->kcj', spectra * signed_half, basis_all, preferred_el...  26.9 us
    dot_general x1, matrix products, body(): jnp.einsum('kcn,kjn->kcj', spectra * live_half, basis_all, preferred_elem...  26.9 us
    dot_general x1, matrix products, body(): jnp.einsum('ljq,ckq->klcj', flux, zonal_table, preferred_element_type=jnp...  26.4 us
    dot_general x1, matrix products, body(): jnp.einsum('kjn,kcj->kcn', basis_all, returned[:, :, half_rows:][:, :, ::...  25.4 us
  transfers between devices with their start and end apart: 4, of which 2 were waited for; matrix products, arithmetic and copies ran while one was open for 5% of the time, Pallas kernels for 0%

commit v1 on v0

v1 whole, which is shorter than its diff:
```python
import functools
import math

import jax
import jax.numpy as jnp
from jax import lax
from jax.experimental import pallas as pl
from jax.experimental.pallas import tpu as pltpu
from jax.sharding import PartitionSpec as P

CHUNKS = 2


def zonal_tables(wavenums, lon):
    columns = jnp.arange(lon, dtype=jnp.int32)
    phases = wavenums[:, None] * columns[None, :] % lon
    angles = phases.astype(jnp.float32) * (2.0 * math.pi / lon)
    table = jnp.concatenate([jnp.cos(angles), jnp.sin(angles)], axis=0)
    return table.astype(jnp.bfloat16)


def zonal_kernel(scale, block, fields_ref, table_ref, out_ref, lines_ref, total_ref):
    my_rows, waves, lanes = fields_ref.shape
    span = lanes // 4

    @pl.when(pl.program_id(0) == 0)
    def _():
        total_ref[...] = jnp.zeros_like(total_ref)
        for j in range(my_rows):
            turned = fields_ref[j].astype(jnp.float32).T.astype(jnp.bfloat16)
            for g in range(2):
                for c in range(2):
                    part = turned[(2 * g + c) * span : (2 * g + c + 1) * span]
                    lines_ref[g, pl.ds(j * span, span), pl.ds(c * waves, waves)] = part

    @pl.loop(0, total_ref.shape[0] // block)
    def _(i):
        rows = pl.ds(pl.multiple_of(i * block, block), block)
        table = table_ref[...]
        wind = jnp.dot(lines_ref[0, rows, :], table, preferred_element_type=jnp.float32)
        vort = jnp.dot(lines_ref[1, rows, :], table, preferred_element_type=jnp.float32)
        flux = (wind * vort).astype(jnp.bfloat16)
        total_ref[rows, :] += lax.dot_general(
            flux, table, (((1,), (1,)), ((), ())), preferred_element_type=jnp.float32
        )

    @pl.when(pl.program_id(0) == pl.num_programs(0) - 1)
    def _():
        for j in range(my_rows):
            rows = total_ref[pl.ds(j * span, span), :] * scale
            both = jnp.concatenate([rows[:, :waves], rows[:, waves:]], axis=0)
            out_ref[j] = both.T.astype(jnp.bfloat16)


def zonal(fields, table):
    my_rows, waves, lanes = fields.shape
    span = lanes // 4
    lines = my_rows * span
    depth, lon = table.shape
    tile = math.gcd(lon, 256)
    block = math.gcd(lines, 320)
    return pl.pallas_call(
        functools.partial(zonal_kernel, 1.0 / math.sqrt(lon), block),
        grid=(lon // tile,),
        in_specs=[
            pl.BlockSpec((my_rows, waves, lanes), lambda i: (0, 0, 0)),
            pl.BlockSpec((depth, tile), lambda i: (0, i)),
        ],
        out_specs=pl.BlockSpec((my_rows, waves, 2 * span), lambda i: (0, 0, 0)),
        out_shape=jax.ShapeDtypeStruct((my_rows, waves, 2 * span), jnp.bfloat16),
        scratch_shapes=[
            pltpu.VMEM((2, lines, depth), jnp.bfloat16),
            pltpu.VMEM((lines, depth), jnp.float32),
        ],
        compiler_params=pltpu.CompilerParams(vmem_limit_bytes=40 * 1024 * 1024),
        cost_estimate=pl.CostEstimate(
            flops=6 * lines * depth * lon,
            bytes_accessed=6 * lines * depth + 2 * depth * lon,
            transcendentals=0,
        ),
    )(fields, table)


def body(assign, u_spec, v_spec, basis):
    slots, lev_dev, _, degrees = u_spec.shape
    rows = basis.shape[1]
    waves = assign.shape[0]
    lat_count = lax.axis_size("lat")
    lev_count = lax.axis_size("lev")
    lon = 4 * rows * lev_count
    lat_index = lax.axis_index("lat")
    lev_index = lax.axis_index("lev")
    step = lev_dev // CHUNKS
    levels = step * lev_count
    row_groups = math.gcd(lat_count, rows)
    lev_groups = lat_count // row_groups
    my_rows = rows // row_groups
    my_levels = levels // lev_groups

    my_waves = lax.dynamic_slice_in_dim(assign, lat_index * slots, slots)
    degree = jnp.arange(degrees, dtype=jnp.int32)
    live_mask = (degree[None, :] >= my_waves[:, None]).astype(jnp.int32)
    signed = live_mask * (1 - 2 * ((degree[None, :] + my_waves[:, None]) % 2))
    masks = jnp.stack([live_mask, signed], axis=1)
    masks_half = masks.astype(jnp.bfloat16)
    masks_full = masks.astype(jnp.float32)
    wave_sign = (1 - 2 * (my_waves % 2)).astype(jnp.float32)[:, None, None]
    parity = (1 - 2 * ((degree[None, :] + my_waves[:, None]) % 2)).astype(jnp.float32)
    parity = parity[:, None, :]
    slope = jnp.sin(my_waves.astype(jnp.float32) * (2.0 * math.pi / lon))
    slope = slope[:, None, None, None, None]

    forward = [(i, i + 1) for i in range(lev_count - 1)]
    backward = [(t, s) for s, t in forward]
    low = lax.ppermute(basis[:, -1:], "lev", forward).astype(jnp.float32)
    high = lax.ppermute(basis[:, :1], "lev", backward).astype(jnp.float32)
    wide = basis.astype(jnp.float32)
    low = jnp.where(lev_index == 0, -wave_sign * wide[:, :1], low)
    high = jnp.where(lev_index == lev_count - 1, parity * wide[:, -1:], high)
    above = jnp.concatenate([low, wide[:, :-1]], axis=1)
    below = jnp.concatenate([wide[:, 1:], high], axis=1)
    slant = (above - below).astype(jnp.bfloat16)
    table = zonal_tables(assign, lon)

    gathered = []
    for i in range(CHUNKS):
        both = [x[:, i * step : (i + 1) * step] for x in (u_spec, v_spec)]
        part = jnp.stack(both, axis=1).transpose(0, 1, 3, 2, 4)
        part = part.reshape(slots, 4 * step, degrees)
        gathered.append(lax.all_gather(part, "lev", axis=0))

    side = jnp.array([-0.5, 0.5], jnp.bfloat16)[:, None, None]
    arrived = []
    for i in range(CHUNKS):
        part = gathered[i].reshape(lev_count, slots, 2, 2, step, degrees)
        part = part.transpose(1, 2, 3, 0, 4, 5).reshape(slots, 2, 2, 1, levels, degrees)
        part = part * masks_half[:, None, None, :, None, :]
        wind = part[:, 0]
        other = part[:, 1].astype(jnp.float32) * slope
        merid = jnp.stack([other[:, 1], -other[:, 0]], axis=1).astype(jnp.bfloat16)
        tilt = wind * side
        head = jnp.stack([wind, merid], axis=1).reshape(slots, 8 * levels, degrees)
        tail = tilt.reshape(slots, 4 * levels, degrees)
        straight = jnp.einsum("kjn,krn->kjr", basis, head, preferred_element_type=jnp.float32)
        turned = jnp.einsum("kjn,krn->kjr", slant, tail, preferred_element_type=jnp.float32)
        send = straight + jnp.pad(turned, ((0, 0), (0, 0), (4 * levels, 0)))
        send = send.astype(jnp.bfloat16).transpose(1, 0, 2)
        if lev_groups > 1:
            send = send.reshape(row_groups, my_rows, slots, 8, lev_groups, my_levels)
            send = send.transpose(0, 4, 1, 2, 3, 5)
        send = send.reshape(lat_count, my_rows, slots, 8 * my_levels)
        arrived.append(lax.all_to_all(send, "lat", split_axis=0, concat_axis=0, tiled=True))

    backs = []
    for i in range(CHUNKS):
        block = arrived[i].transpose(1, 0, 2, 3).reshape(my_rows, waves, 8 * my_levels)
        backs.append(zonal(block, table))
    back = jnp.concatenate(backs, axis=2).reshape(my_rows, lat_count, slots, -1)
    back = back.transpose(1, 0, 2, 3)
    block = lax.all_to_all(back, "lat", split_axis=0, concat_axis=0, tiled=True)
    if lev_groups > 1:
        block = block.reshape(row_groups, lev_groups, my_rows, slots, 4 * CHUNKS, my_levels)
        block = block.transpose(0, 2, 3, 4, 1, 5)
    block = block.reshape(rows, slots, CHUNKS * 4 * levels).transpose(1, 0, 2)

    results = []
    for i in range(CHUNKS):
        part = block[:, :, i * 4 * levels : (i + 1) * 4 * levels]
        product = jnp.einsum("kjr,kjn->krn", part, basis, preferred_element_type=jnp.float32)
        product = product.reshape(slots, 2, 2, levels, degrees)
        total = (
            product[:, :, 0] * masks_full[:, None, :1, :]
            + product[:, :, 1] * masks_full[:, None, 1:, :]
        )
        total = total.astype(jnp.bfloat16).reshape(slots, 2, lev_count, step, degrees)
        total = total.transpose(2, 1, 3, 0, 4).reshape(lev_count * 2 * step, slots * degrees)
        total = lax.psum_scatter(total, "lev", scatter_dimension=0, tiled=True)
        results.append(total.reshape(2, step, slots, degrees))
    result = jnp.concatenate(results, axis=1).transpose(2, 1, 0, 3)
    return result.astype(jnp.float32)


def solution(mesh):
    return jax.shard_map(
        body,
        mesh=mesh,
        in_specs=(
            P(),
            P("lat", "lev", None, None),
            P("lat", "lev", None, None),
            P("lat", "lev", None),
        ),
        out_specs=P("lat", "lev", None, None),
        check_vma=False,
    )
```

time: 1050 us -> 724 us (0.69)
  waiting for transfers between devices: 581 us -> 215 us
  blocking collectives: 119 us -> 0 us
  other arithmetic: 40 us -> 136 us
  local copies, waits for them, and re-layouts: 125 us -> 207 us
  matrix products: 151 us -> 83 us
  Pallas kernels: 0 us -> 43.5 us
    all_gather x1 -> x2, waiting for transfers between devices: 381 us -> 0.01 us  [body(): gathered.append(lax.all_gather(part, 'lev', axis=0))]
    all_to_all x1 -> x0, blocking collectives: 119 us -> none  [body(): lax.all_to_all(zonal_back, 'lat', split_axis=0, concat_axis=2, tiled=True)]
    reduce_scatter x0 -> x2, waiting for transfers between devices: none -> 74.2 us  [body(): total = lax.psum_scatter(total, 'lev', scatter_dimension=0, tiled=True)]
    slice x5 -> x10, local copies, waits for them, and re-layouts: 21.9 us -> 95.7 us  [the longest x1 43.3 us: body(): below = jnp.concatenate([wide[:, 1:], high], axis=1)]
    dot_general x6, matrix products: 151 us -> 83 us  [the longest x2 27.9 us: body(): jnp.einsum('kjn,krn->kjr', slant, tail, preferred_element_type=jnp.float32)]
    all_to_all x1 -> x3, waiting for transfers between devices: 200 us -> 140 us  [the longest x1 72.2 us: body(): block = lax.all_to_all(back, 'lat', split_axis=0, concat_axis=0, tiled=True)]
    convert_element_type x2 -> x5, other arithmetic: 1.65 us -> 50.2 us  [the longest x1 27.4 us: body(): slant = (above - below).astype(jnp.bfloat16)]
    pallas_call x0 -> x2, Pallas kernels: none -> 43.5 us  [zonal(): pl.pallas_call(functools.partial(zonal_kernel, 1.0 / math.sqrt(lon), bloc...]
  transfers between devices with their start and end apart: 4 -> 9, of which waited for: 2 -> 5; matrix products, arithmetic and copies ran while one was open for 5% -> 27% of each run, Pallas kernels for 0% -> 0%
where the time goes in v1:
time: 724 us; the launch traced here: 720 us
  waiting for transfers between devices  215 us (30%)
  local copies, waits for them, and re-layouts  207 us (29%)
  other arithmetic  136 us (19%)
  matrix products  83 us (11%)
  Pallas kernels  43.5 us (6%)
  starting transfers between devices  21.5 us (3%)
  between operations  13.8 us (2%)
    reduce_scatter x2, waiting for transfers between devices, body(): total = lax.psum_scatter(total, 'lev', scatter_dimension=0, tiled=True)  74.2 us
    all_to_all x1, waiting for transfers between devices, body(): block = lax.all_to_all(back, 'lat', split_axis=0, concat_axis=0, tiled=True)  72.2 us
    all_to_all x2, waiting for transfers between devices, body(): lax.all_to_all(send, 'lat', split_axis=0, concat_axis=0, tiled=True)  68.3 us
    pallas_call x2, Pallas kernels, zonal(): pl.pallas_call(functools.partial(zonal_kernel, 1.0 / math.sqrt(lon), bloc...  43.5 us
    unnamed x42, local copies, waits for them, and re-layouts  43.5 us
    slice x1, local copies, waits for them, and re-layouts, body(): below = jnp.concatenate([wide[:, 1:], high], axis=1)  43.3 us
    another operation x1, other arithmetic  28 us
    dot_general x2, matrix products, body(): jnp.einsum('kjn,krn->kjr', slant, tail, preferred_element_type=jnp.float32)  27.9 us
  transfers between devices with their start and end apart: 9, of which 5 were waited for; matrix products, arithmetic and copies ran while one was open for 27% of the time, Pallas kernels for 0%

profile of v1, /device:TPU:0, one launch (start us, length us, event | category | flops | bytes accessed | tf_op | source)
XLA Modules:
  0.0 719.7 jit_solution(12812973299997039112)
XLA Ops:
  23.2 21.7 %copy_convert_fusion = f32[80,160,640]{2,0,1:T(8,128)} fusion(bf16[80,160,640]{2,1,0:T(8,128)(2,1)} %param.8), kind=kLoop, calls=%fused_computation.91 | loop fusion | flops 8192000 | bytes 49152000 | tf_op jit(solution)/shard_map/convert_element_type | solution.py:117
  45.0 43.3 %fusion.47 = (f32[80,159,640]{2,0,1:T(8,128)}, f32[80,159,640]{2,0,1:T(8,128)}) fusion(f32[80,160,640]{2,0,1:T(8,128)} %copy_convert_fusion), kind=kLoop, calls=%fused_computation.92 | loop fusion | bytes 130252800 | tf_op jit(solution)/shard_map/slice | solution.py:121
  90.6 27.4 %fusion = bf16[80,160,640]{2,0,1:T(8,128)(2,1)} fusion(f32[80,159,640]{2,0,1:T(8,128)} %get-tuple-element.8, f32[80,1,640]{2,0,1:T(8,128)S(1)} %get-tuple-element.10, f32[80,1,640]{2,0,1:T(8,128)S(1)} %get-tuple-element.9, f32[80,159,640]{2,0,1:T(8,128)} %get-tuple-element.7), kind=kLoop, calls=%fused_computation.1 | loop fusion | flops 32768000 | bytes 81920000 | tf_op jit(solution)/shard_map/convert_element_type | solution.py:122
  136.1 11.5 %broadcast_multiply_fusion.1 = (bf16[80,2,2,2,16,640]{5,4,3,0,2,1:T(8,128)(2,1)S(1)}, bf16[80,2,2,2,16,640]{5,4,3,0,2,1:T(8,128)(2,1)}) fusion(bf16[80,2,640]{2,1,0:T(2,128)(2,1)S(1)} %copy.80, bf16[80,2,2,16,640]{4,3,0,2,1:T(8,128)(2,1)} %copy.79, bf16[80,2,2,16,640]{4,3,0,2,1:T(8,128)(2,1)} %copy.96), kind=kLoop, calls=%fused_computation.36 | loop fusion | flops 13107200 | bytes 39526400 | tf_op jit(solution)/shard_map/mul | solution.py:137
  147.5 10.8 %slice.118 = bf16[80,1,2,2,16,640]{5,4,3,0,2,1:T(8,128)(2,1)} slice(bf16[80,2,2,2,16,640]{5,4,3,0,2,1:T(8,128)(2,1)} %get-tuple-element.28), slice={[0:80], [0:1], [0:2], [0:2], [0:16], [0:640]} | slice | bytes 13107200 | tf_op jit(solution)/shard_map/slice | solution.py:138
  158.4 11.8 %convert_multiply_fusion.1 = (f32[80,2,2,16,640]{4,3,2,0,1:T(8,128)}, f32[80,2,2,16,640]{4,3,2,0,1:T(8,128)}) fusion(bf16[80,2,2,2,16,640]{5,4,3,0,2,1:T(8,128)(2,1)S(1)} %get-tuple-element.27, f32[80]{0:T(128)S(1)} %get-tuple-element.5, bf16[80,2,2,2,16,640]{5,4,3,0,2,1:T(8,128)(2,1)} %get-tuple-element.28), kind=kLoop, calls=%fused_computation.9 | loop fusion | flops 13107200 | bytes 39321920 | tf_op jit(solution)/shard_map/mul | solution.py:139
  197.9 5.8 copy.97
  203.7 14.0 %fusion.1 = f32[80,160,64]{2,1,0:T(8,128)} fusion(bf16[80,160,640]{2,0,1:T(8,128)(2,1)} %fusion, bf16[80,64,640]{2,1,0:T(8,128)(2,1)} %bitcast.139, bf16[64]{0:T(256)(128)(2,1)S(1)} %mul.177), kind=kOutput, calls=%fused_computation.2 | convolution fusion | flops 1051852800 | bytes 26214528 | tf_op jit(solution)/shard_map/kjn,krn->kjr/dot_general | solution.py:145
  217.7 14.0 %fusion.19 = bf16[160,80,128]{2,0,1:T(8,128)(2,1)S(1)} fusion(f32[80,160,64]{2,1,0:T(8,128)} %fusion.1, bf16[80,128,640]{2,1,0:T(8,128)(2,1)} %bitcast.113, bf16[80,160,640]{2,1,0:T(8,128)(2,1)} %param.8), kind=kOutput, calls=%fused_computation.41 | convolution fusion | flops 2100428800 | bytes 36044800 | tf_op jit(solution)/shard_map/kjn,krn->kjr/dot_general | solution.py:144
  234.7 7.6 %all-to-all-start.1 = ((bf16[8,20,80,128]{3,2,1,0:T(8,128)(2,1)}), bf16[8,20,80,128]{3,2,1,0:T(8,128)(2,1)}, u32[]{:S(2)}, u32[]{:S(2)}) async-start(bf16[8,20,80,128]{3,2,1,0:T(8,128)(2,1)} %bitcast.131), calls=%async_computation.1 | async-start | bytes 6553600 | tf_op jit(solution)/shard_map/all_to_all | solution.py:152
  242.3 6.9 copy.86
  249.3 9.0 %maximum_maximum_fusion = bf16[80,2,2,2,16,640]{5,4,3,2,1,0:T(8,128)(2,1)} fusion(bf16[80,1,1,2,16,640]{5,4,3,2,1,0:T(8,128)(2,1)S(1)} %copy-done.4, bf16[80,1,1,2,16,640]{5,4,3,2,1,0:T(8,128)(2,1)S(1)} %copy-done.5, bf16[80,2,2,2,16,640]{5,4,3,0,2,1:T(8,128)(2,1)} %copy-done.1), kind=kLoop, calls=%fused_computation.6 | loop fusion | flops 39321600 | bytes 26214400 | tf_op jit(solution)/shard_map/stack | solution.py:142
  258.3 14.0 %fusion.3 = f32[80,160,64]{2,1,0:T(8,128)} fusion(bf16[80,160,640]{2,0,1:T(8,128)(2,1)} %fusion, bf16[80,64,640]{2,1,0:T(8,128)(2,1)} %bitcast.138, bf16[64]{0:T(256)(128)(2,1)S(1)} %mul.177), kind=kOutput, calls=%fused_computation.4 | convolution fusion | flops 1051852800 | bytes 26214528 | tf_op jit(solution)/shard_map/kjn,krn->kjr/dot_general | solution.py:145
  272.2 13.8 %fusion.18 = bf16[160,80,128]{2,0,1:T(8,128)(2,1)S(1)} fusion(f32[80,160,64]{2,1,0:T(8,128)} %fusion.3, bf16[80,128,640]{2,1,0:T(8,128)(2,1)} %bitcast.112, bf16[80,160,640]{2,1,0:T(8,128)(2,1)} %param.8), kind=kOutput, calls=%fused_computation.40 | convolution fusion | flops 2100428800 | bytes 36044800 | tf_op jit(solution)/shard_map/kjn,krn->kjr/dot_general | solution.py:144
  289.2 27.0 %all-to-all-done.1 = bf16[8,20,80,128]{3,2,1,0:T(8,128)(2,1)} async-done(((bf16[8,20,80,128]{3,2,1,0:T(8,128)(2,1)}), bf16[8,20,80,128]{3,2,1,0:T(8,128)(2,1)}, u32[]{:S(2)}, u32[]{:S(2)}) %all-to-all-start.1) | async-done | bytes 3276832 | tf_op jit(solution)/shard_map/all_to_all | solution.py:152
  321.4 28.0 %cosine_convert_fusion = (bf16[640,2560]{1,0:T(8,128)(2,1)S(1)}, bf16[640,2560]{1,0:T(8,128)(2,1)S(1)}) fusion(s32[640]{0:T(1024)S(1)} %copy-done.8), kind=kLoop, calls=%fused_computation.31 | loop fusion | flops 18022400 | bytes 6556160 | tf_op jit(solution)/shard_map/convert.8
  355.4 41.3 %all-to-all-done = bf16[8,20,80,128]{3,2,1,0:T(8,128)(2,1)} async-done(((bf16[8,20,80,128]{3,2,1,0:T(8,128)(2,1)}), bf16[8,20,80,128]{3,2,1,0:T(8,128)(2,1)}, u32[]{:S(2)}, u32[]{:S(2)}) %all-to-all-start) | async-done | bytes 3276832 | tf_op jit(solution)/shard_map/all_to_all | solution.py:152
  400.5 21.8 %shard_map.56 = bf16[20,640,64]{2,1,0:T(8,128)(2,1)S(1)} custom-call(bf16[20,640,128]{2,1,0:T(8,128)(2,1)S(1)} %bitcast.108, bf16[1280,2560]{1,0:T(8,128)(2,1)S(1)} %copy-done), custom_call_target="tpu_custom_call" | custom-call | flops 12582912000 | bytes 11468800 | tf_op jit(solution)/shard_map/pallas_call | solution.py:62
  422.3 21.8 %shard_map.55 = bf16[20,640,64]{2,1,0:T(8,128)(2,1)S(1)} custom-call(bf16[20,640,128]{2,1,0:T(8,128)(2,1)S(1)} %bitcast.109, bf16[1280,2560]{1,0:T(8,128)(2,1)S(1)} %copy-done), custom_call_target="tpu_custom_call" | custom-call | flops 12582912000 | bytes 11468800 | tf_op jit(solution)/shard_map/pallas_call | solution.py:62
  453.7 72.2 %all-to-all-done.2 = bf16[8,20,80,128]{3,2,1,0:T(8,128)(2,1)S(1)} async-done(((bf16[8,20,80,128]{3,2,1,0:T(8,128)(2,1)}), bf16[8,20,80,128]{3,2,1,0:T(8,128)(2,1)S(1)}, u32[]{:S(2)}, u32[]{:S(2)}) %all-to-all-start.2) | async-done | bytes 3276832 | tf_op jit(solution)/shard_map/all_to_all | solution.py:160
  525.8 7.5 %copy.104 = bf16[160,80,128]{0,2,1:T(8,128)(2,1)} copy(bf16[160,80,128]{2,1,0:T(8,128)(2,1)S(1)} %bitcast.137) | data formatting | bytes 6553600 | tf_op jit(solution)/shard_map/reshape | solution.py:164
  533.3 14.1 %fusion.28 = f32[80,64,640]{2,1,0:T(8,128)} fusion(bf16[80,160,640]{2,1,0:T(8,128)(2,1)} %param.8, bf16[80,160,128]{1,2,0:T(8,128)(2,1)} %bitcast.116), kind=kOutput, calls=%fused_computation.53 | convolution fusion | flops 1048576000 | bytes 32112640 | tf_op jit(solution)/shard_map/kjr,kjn->krn/dot_general | solution.py:169
  547.4 13.2 %fusion.26 = f32[80,64,640]{2,1,0:T(8,128)} fusion(bf16[80,160,640]{2,1,0:T(8,128)(2,1)} %param.8, bf16[80,160,128]{1,2,0:T(8,128)(2,1)S(1)} %bitcast.117), kind=kOutput, calls=%fused_computation.51 | convolution fusion | flops 1048576000 | bytes 32112640 | tf_op jit(solution)/shard_map/kjr,kjn->krn/dot_general | solution.py:169
  560.6 10.5 %fusion.49 = (f32[80,2,1,16,640]{4,3,2,1,0:T(8,128)}, f32[80,2,1,16,640]{4,3,2,1,0:T(8,128)}) fusion(f32[80,2,2,16,640]{4,3,2,1,0:T(8,128)} %bitcast.111), kind=kLoop, calls=%fused_computation.94 | loop fusion | bytes 26214400 | tf_op jit(solution)/shard_map/slice | solution.py:172
  571.1 9.4 %copy.119 = f32[80,2,1,16,640]{4,0,3,1,2:T(8,128)} copy(f32[80,2,1,16,640]{4,3,2,1,0:T(8,128)} %get-tuple-element.14) | data formatting | bytes 13107200
  580.6 6.7 copy.118
  587.3 10.5 %fusion.50 = (f32[80,2,1,16,640]{4,3,2,1,0:T(8,128)}, f32[80,2,1,16,640]{4,3,2,1,0:T(8,128)}) fusion(f32[80,2,2,16,640]{4,3,2,1,0:T(8,128)} %bitcast.110), kind=kLoop, calls=%fused_computation.95 | loop fusion | bytes 26214400 | tf_op jit(solution)/shard_map/slice | solution.py:172
  597.8 9.5 %copy.121 = f32[80,2,1,16,640]{4,0,3,1,2:T(8,128)} copy(f32[80,2,1,16,640]{4,3,2,1,0:T(8,128)} %get-tuple-element.16) | data formatting | bytes 13107200
  607.3 9.6 %copy.120 = f32[80,2,1,16,640]{4,0,3,1,2:T(8,128)} copy(f32[80,2,1,16,640]{4,3,2,1,0:T(8,128)} %get-tuple-element.15) | data formatting | bytes 13107200
  617.0 7.4 %fusion.16 = (bf16[4,2,4,80,640]{4,3,2,0,1:T(8,128)(2,1)S(1)}, bf16[4,2,4,80,640]{4,3,2,0,1:T(8,128)(2,1)}) fusion(f32[80,2,4,4,640]{4,0,3,2,1:T(8,128)S(1)} %bitcast.120, f32[80,2,4,4,640]{4,0,3,2,1:T(8,128)S(1)} %bitcast.123, f32[80,640]{1,0:T(8,128)S(1)} %copy-done.7, f32[80,640]{1,0:T(8,128)S(1)} %get-tuple-element.23, ...), kind=kLoop, calls=%fused_computation.38 | loop fusion | flops 13107200 | bytes 33177600 | tf_op jit(solution)/shard_map/transpose | solution.py:176
  631.7 34.3 %reduce-scatter.5.cloned.1.call-done = bf16[8,51200]{1,0:T(8,128)(2,1)} async-done(((bf16[32,51200]{1,0:T(8,128)(2,1)}), bf16[8,51200]{1,0:T(8,128)(2,1)}) %reduce-scatter.5.cloned.1.call-update) | async-done | bytes 819216 | tf_op jit(solution)/shard_map/reduce_scatter | solution.py:177
  667.2 39.9 %reduce-scatter.3.cloned.1.call-done = bf16[8,51200]{1,0:T(8,128)(2,1)} async-done(((bf16[32,51200]{1,0:T(8,128)(2,1)}), bf16[8,51200]{1,0:T(8,128)(2,1)}) %reduce-scatter.3.cloned.1.call-update) | async-done | bytes 819216 | tf_op jit(solution)/shard_map/reduce_scatter | solution.py:177
  (100 shorter events, 109.5 us)
Async XLA Ops:
  6.5 111.5 %all-gather.3.cloned.1.call-start = ((), (), s32[]{:S(2)}) async-start(), calls=%async_computation.5 | async-start | bytes 8192000 | tf_op jit(solution)/shard_map/all_gather | solution.py:130
  13.7 113.3 %all-gather.5.cloned.1.call-start = ((), (), s32[]{:S(2)}) async-start(), calls=%async_computation.6 | async-start | bytes 8192000 | tf_op jit(solution)/shard_map/all_gather | solution.py:130
  17.2 72.2 %collective-permute-start.1 = (bf16[80,1,640]{2,0,1:T(8,128)(2,1)S(1)}, bf16[80,1,640]{2,0,1:T(8,128)(2,1)S(1)}, u32[]{:S(2)}, u32[]{:S(2)}) collective-permute-start(bf16[80,1,640]{2,0,1:T(8,128)(2,1)S(1)} %copy.137), channel_id=1, source_target_pairs={{1,0},{2,1},{3,2},{5,4},{6,5},{7,6},{9,8},{10,9},{11,10},{13,12},{... | collective-permute-start | bytes 307208 | tf_op jit(solution)/shard_map/ppermute | solution.py:116
  18.6 70.8 %collective-permute-start = (bf16[80,1,640]{2,0,1:T(8,128)(2,1)S(1)}, bf16[80,1,640]{2,0,1:T(8,128)(2,1)S(1)}, u32[]{:S(2)}, u32[]{:S(2)}) collective-permute-start(bf16[80,1,640]{2,0,1:T(8,128)(2,1)S(1)} %copy.136), channel_id=1, source_target_pairs={{0,1},{1,2},{2,3},{4,5},{5,6},{6,7},{8,9},{9,10},{10,11},{12,13},{... | collective-permute-start | bytes 307208 | tf_op jit(solution)/shard_map/ppermute | solution.py:115
  45.0 44.3 %copy-start.9 = (bf16[2]{0:T(256)(128)(2,1)S(1)}, bf16[2]{0:T(256)(128)(2,1)}, u32[]{:S(2)}) copy-start(bf16[2]{0:T(256)(128)(2,1)} %constant.65.clone) | copy-start | bytes 16
  147.5 31.3 %copy-start.1 = (bf16[80,2,2,2,16,640]{5,4,3,0,2,1:T(8,128)(2,1)}, bf16[80,2,2,2,16,640]{5,4,3,0,2,1:T(8,128)(2,1)S(1)}, u32[]{:S(2)}) copy-start(bf16[80,2,2,2,16,640]{5,4,3,0,2,1:T(8,128)(2,1)S(1)} %get-tuple-element.27) | copy-start | bytes 39321604
  182.0 10.4 %slice-start = ((s8[6553600]{0:T(1024)(128)(4,1)}), s8[4194304]{0:T(1024)(128)(4,1)S(1)}, s32[]{:S(2)}) async-start(s8[6553600]{0:T(1024)(128)(4,1)} %bitcast.114), calls=%async_computation.9 | async-start | bytes 8388608
  182.0 10.4 %slice-start.1 = ((s8[6553600]{0:T(1024)(128)(4,1)}), s8[2359296]{0:T(1024)(128)(4,1)S(1)}, s32[]{:S(2)}) async-start(s8[6553600]{0:T(1024)(128)(4,1)} %bitcast.114), calls=%async_computation.10 | async-start | bytes 4718592
  192.5 3.7 copy-start.6
  234.7 81.5 %all-to-all-start.1 = ((bf16[8,20,80,128]{3,2,1,0:T(8,128)(2,1)}), bf16[8,20,80,128]{3,2,1,0:T(8,128)(2,1)}, u32[]{:S(2)}, u32[]{:S(2)}) async-start(bf16[8,20,80,128]{3,2,1,0:T(8,128)(2,1)} %bitcast.131), calls=%async_computation.1 | async-start | bytes 6553600 | tf_op jit(solution)/shard_map/all_to_all | solution.py:152
  242.3 6.9 copy-start.4
  242.3 6.9 copy-start.5
  286.1 35.3 %copy-start.8 = (s32[640]{0:T(1024)S(1)}, s32[640]{0:T(1024)}, u32[]{:S(2)}) copy-start(s32[640]{0:T(1024)} %param.5) | copy-start | bytes 7684
  316.1 80.5 %all-to-all-start = ((bf16[8,20,80,128]{3,2,1,0:T(8,128)(2,1)}), bf16[8,20,80,128]{3,2,1,0:T(8,128)(2,1)}, u32[]{:S(2)}, u32[]{:S(2)}) async-start(bf16[8,20,80,128]{3,2,1,0:T(8,128)(2,1)} %bitcast.132), calls=%async_computation | async-start | bytes 6553600 | tf_op jit(solution)/shard_map/all_to_all | solution.py:152
  396.7 3.8 copy-start
  448.2 77.7 %all-to-all-start.2 = ((bf16[8,20,80,128]{3,2,1,0:T(8,128)(2,1)}), bf16[8,20,80,128]{3,2,1,0:T(8,128)(2,1)S(1)}, u32[]{:S(2)}, u32[]{:S(2)}) async-start(bf16[8,20,80,128]{3,2,1,0:T(8,128)(2,1)} %bitcast.107), calls=%async_computation.2 | async-start | bytes 6553600 | tf_op jit(solution)/shard_map/all_to_all | solution.py:160
  451.8 214.2 %reduce-scatter.5.cloned.1.call-start = ((), (), s32[]{:S(2)}) async-start(), calls=%async_computation.8 | async-start | bytes 4096000 | tf_op jit(solution)/shard_map/reduce_scatter | solution.py:177
  533.3 14.1 %copy-start.2 = (bf16[160,80,128]{0,2,1:T(8,128)(2,1)S(1)}, bf16[160,80,128]{0,2,1:T(8,128)(2,1)}, u32[]{:S(2)}) copy-start(bf16[160,80,128]{0,2,1:T(8,128)(2,1)} %copy.104) | copy-start | bytes 9830404
  571.1 9.5 %copy-start.3 = (f32[80,2,1,16,640]{4,3,2,1,0:T(8,128)S(1)}, f32[80,2,1,16,640]{4,3,2,1,0:T(8,128)}, u32[]{:S(2)}) copy-start(f32[80,2,1,16,640]{4,3,2,1,0:T(8,128)} %get-tuple-element.13) | copy-start | bytes 19660804
  597.8 19.1 %slice-start.2 = ((s8[6553600]{0:T(1024)(128)(4,1)}), s8[4194304]{0:T(1024)(128)(4,1)S(1)}, s32[]{:S(2)}) async-start(s8[6553600]{0:T(1024)(128)(4,1)} %bitcast.118), calls=%async_computation.11 | async-start | bytes 8388608
  597.8 19.1 %slice-start.4 = ((s8[6553600]{0:T(1024)(128)(4,1)}), s8[4194304]{0:T(1024)(128)(4,1)S(1)}, s32[]{:S(2)}) async-start(s8[6553600]{0:T(1024)(128)(4,1)} %bitcast.121), calls=%async_computation.13 | async-start | bytes 8388608
  607.3 9.6 %slice-start.3 = ((s8[6553600]{0:T(1024)(128)(4,1)}), s8[2359296]{0:T(1024)(128)(4,1)S(1)}, s32[]{:S(2)}) async-start(s8[6553600]{0:T(1024)(128)(4,1)} %bitcast.118), calls=%async_computation.12 | async-start | bytes 4718592
  607.3 9.6 %slice-start.5 = ((s8[6553600]{0:T(1024)(128)(4,1)}), s8[2359296]{0:T(1024)(128)(4,1)S(1)}, s32[]{:S(2)}) async-start(s8[6553600]{0:T(1024)(128)(4,1)} %bitcast.121), calls=%async_computation.14 | async-start | bytes 4718592
  607.3 9.6 %copy-start.7 = (f32[80,640]{1,0:T(8,128)S(1)}, f32[80,640]{1,0:T(8,128)}, u32[]{:S(2)}) copy-start(f32[80,640]{1,0:T(8,128)} %get-tuple-element.24) | copy-start | bytes 614404
  629.0 78.1 %reduce-scatter.3.cloned.1.call-start = ((), (), s32[]{:S(2)}) async-start(), calls=%async_computation.7 | async-start | bytes 4096000 | tf_op jit(solution)/shard_map/reduce_scatter | solution.py:177
Sparse Core Ops, SparseCore 0:
  13.9 50.5 all-gather.2
  66.0 48.0 all-gather.4
  629.1 36.8 reduce-scatter.4
  668.4 38.6 reduce-scatter.2
